TPU v7x, 32 devices: a whole 2x2x4 slice. The times are simulated.
32 devices in a mesh: seq: 8 (over z, x), head: 4 (over y, core).
Axes of the slice: x: 2, y: 2, z: 4, core: 2. Of those that a mesh axis runs over, the one named last changes fastest.
Arguments:
- video_q: bfloat16 [1024, 4096], P(('seq', 'head')), may hold values from -200 to 200
- video_k: bfloat16 [1024, 4096], P(('seq', 'head')), may hold values from -6 to 6
- video_v: bfloat16 [1024, 4096], P(('seq', 'head')), may hold values from -6 to 6
- text_k: bfloat16 [512, 4096], P(None, 'head'), may hold values from -6 to 6
- text_v: bfloat16 [512, 4096], P(None, 'head'), may hold values from -6 to 6
- out_weight: bfloat16 [4096, 5120], P('head'), may hold values from -0.09375 to 0.09375
Outputs:
- video_out: bfloat16 [1024, 5120], P(('seq', 'head'))
All inputs are finite; a program needn't handle non-finite values.
Results may differ from a plain program's by a relative error of at most 0.018.
Values may be sent and summed in bfloat16 or wider, within the bound.
A program may use at most 128 MiB of HBM per device.

v0:
```python
import functools
import math

import jax
import jax.numpy as jnp
from jax import lax
from jax.experimental import pallas as pl
from jax.experimental.pallas import tpu as pltpu
from jax.sharding import PartitionSpec as P

HD = 128
BF16 = jnp.bfloat16
F32 = jnp.float32
CORES = 2
SCALE = HD ** (-0.5) * math.log2(math.e)


def kernel(
    n_seq, n_head, q_ref, k_ref, v_ref, tk_ref, tv_ref, w_ref, o_ref,
    stage, keys_in, vals, queries, tk, tv, w, probs, att_send, att, part, pair_in, y_send, y_in,
    load_sem, text_sem, w_sem, k_send, k_recv, v_send, v_recv, q_send, q_recv,
    att_ssem, att_rsem, pair_ssem, pair_rsem, y_ssem, y_rsem,
):
    s, g = lax.axis_index("seq"), lax.axis_index("head")
    core, chip = lax.rem(g, CORES), lax.div(g, CORES)
    chips = n_head // CORES
    rows = q_ref.shape[0]
    n_cols = w_sem.shape[0]
    width = w_ref.shape[1] // n_cols
    per_chunk = probs.shape[1] // rows
    chunks = n_seq // per_chunk
    split = n_seq * n_head * rows

    def lanes(block):
        return pl.ds(pl.multiple_of(block * HD, HD), HD)

    def cols(n):
        return pl.ds(n * width, width)

    loads = [
        pltpu.make_async_copy(ref, stage.at[i], load_sem.at[i])
        for i, ref in enumerate((k_ref, q_ref, v_ref))
    ]
    texts = [
        pltpu.make_async_copy(tk_ref.at[:, lanes(s)], tk, text_sem.at[0]),
        pltpu.make_async_copy(tv_ref.at[:, lanes(s)], tv, text_sem.at[1]),
    ]
    weights = [
        pltpu.make_async_copy(w_ref.at[:, cols(n)], w.at[:, cols(n)], w_sem.at[n])
        for n in range(n_cols)
    ]
    for copy in loads + texts + weights:
        copy.start()

    turns = list(range(1, chips)) + [0]
    offsets = list(range(n_seq))

    def targets(turn):
        return [
            (lax.rem(s + o, n_seq), lax.rem(chip + chips - turn, chips) * CORES + lax.rem(core + c, CORES))
            for o in offsets for c in range(CORES) if (turn, o, c) != (0, 0, 0)
        ]

    others = [
        (lax.rem(s + o, n_seq), lax.rem(chip + chips - turn, chips) * CORES + lax.rem(core + c, CORES))
        for o in offsets for turn in turns for c in range(CORES) if (turn, o, c) != (0, 0, 0)
    ]
    barrier = pltpu.get_barrier_semaphore()
    for ts, tg in others:
        pl.semaphore_signal(
            barrier, inc=1, device_id={"seq": ts, "head": tg},
            device_id_type=pl.DeviceIdType.MESH,
        )
    pl.semaphore_wait(barrier, len(others))

    def send(src, dst, ssem, rsem, ts, tg):
        return pltpu.make_async_remote_copy(
            src_ref=src, dst_ref=dst, send_sem=ssem, recv_sem=rsem,
            device_id={"seq": ts, "head": tg}, device_id_type=pl.DeviceIdType.MESH,
        )

    def wait_for(ref, sem):
        pltpu.make_async_copy(ref, ref, sem).wait()

    mine = lanes(g * n_seq + s)

    def spread(i, buffer, ssem, rsem, to):
        for ts, tg in to:
            send(stage.at[i, :, lanes(tg * n_seq + ts)], buffer.at[s, g], ssem, rsem, ts, tg).start()

    loads[0].wait()
    spread(0, keys_in, k_send, k_recv, others)
    pltpu.make_async_copy(stage.at[0, :, mine], keys_in.at[s, g], k_recv).start()
    loads[1].wait()
    for turn in turns[:-1]:
        spread(1, queries, q_send.at[turn], q_recv.at[turn], targets(turn))
    loads[2].wait()
    spread(2, vals, v_send, v_recv, others)
    pltpu.make_async_copy(stage.at[2, :, mine], vals.at[s, g], v_recv).start()
    spread(1, queries, q_send.at[0], q_recv.at[0], targets(0))
    pltpu.make_async_copy(stage.at[1, :, mine], queries.at[s, g], q_recv.at[0]).start()

    texts[0].wait()
    wait_for(keys_in, k_recv)
    keyed = (((1,), (1,)), ((), ()))
    group = lax.div(s, per_chunk)
    blocks = [lax.rem(group + c + 1, chunks) * per_chunk for c in range(chunks)]
    owners = [(t, lax.rem(chip + t, chips)) for t in turns]
    passes = [(t, owner, cc) for t, owner in owners for cc in range(CORES)]
    for order, (t, owner, cc) in enumerate(passes):
        if cc == 0:
            wait_for(queries.at[:, pl.ds(owner * CORES, CORES)], q_recv.at[t])
        for c, first in enumerate(blocks):
            q = queries[pl.ds(first, per_chunk), owner * CORES + cc].reshape(per_chunk * rows, HD)
            keys = keys_in[...].reshape(split, HD)
            on_video = lax.dot_general(q, keys, keyed, preferred_element_type=F32)
            on_text = lax.dot_general(q, tk[...], keyed, preferred_element_type=F32)
            top = jnp.maximum(
                jnp.max(on_video, axis=1, keepdims=True),
                jnp.max(on_text, axis=1, keepdims=True),
            )
            probs[c, :, :split] = jnp.exp2((on_video - top) * SCALE).astype(BF16)
            probs[c, :, split:] = jnp.exp2((on_text - top) * SCALE).astype(BF16)
        if order == 0:
            texts[1].wait()
            wait_for(vals, v_recv)
        for c, first in enumerate(blocks):
            values = vals[...].reshape(split, HD)
            ahead = jnp.dot(
                probs[c, :, :split],
                jnp.concatenate([values, jnp.ones_like(values)], axis=1),
                preferred_element_type=F32,
            ) + jnp.dot(
                probs[c, :, split:],
                jnp.concatenate([tv[...], jnp.ones_like(tv)], axis=1),
                preferred_element_type=F32,
            )
            done = (ahead[:, :HD] / ahead[:, HD:]).astype(BF16)
            att_send[t, cc, c] = done.reshape(per_chunk, rows, HD)
            for b in range(per_chunk):
                here = lax.rem(s + b, per_chunk) if c == chunks - 1 else b
                src, dst = att_send.at[t, cc, c, here], att.at[t, cc, :, lanes(s)]
                if c == chunks - 1 and b == 0:
                    pltpu.make_async_copy(src, dst, att_rsem.at[t, cc]).start()
                else:
                    send(src, dst, att_ssem.at[t, cc], att_rsem.at[t, cc], first + here, g).start()

    def to_pair(t, n):
        return send(
            part.at[t, 1 - core, :, cols(n)], pair_in.at[t, :, cols(n)],
            pair_ssem.at[t, n], pair_rsem.at[t, n], s, g + 1 - 2 * core,
        )

    def to_owner(t, owner, n):
        return send(
            y_send.at[t - 1, :, cols(n)], y_in.at[t - 1, :, cols(n)],
            y_ssem.at[t - 1, n], y_rsem.at[t - 1, n], s, owner * CORES + core,
        )

    def own_sum(t, n):
        to_pair(t, n).wait_recv()
        return part[t, core, :, cols(n)].astype(F32) + pair_in[t, :, cols(n)].astype(F32)

    def cross(t, owner, cc, n):
        @pl.when(core == cc)
        def _():
            y_send[t - 1, :, cols(n)] = own_sum(t, n).astype(BF16)
            to_owner(t, owner, n).start()

    LAG = 2
    pending = []
    for order, (t, owner, cc) in enumerate(passes):
        wait_for(att.at[t, cc], att_rsem.at[t, cc])
        for n in range(n_cols):
            if order == 0:
                weights[n].wait()
            part[t, cc, :, cols(n)] = jnp.dot(
                att[t, cc], w[:, cols(n)], preferred_element_type=F32
            ).astype(BF16)

            @pl.when(core != cc)
            def _():
                to_pair(t, n).start()

            if t > 0:
                pending.append((t, owner, cc, n))
            if pending and (len(pending) > LAG or t == 0):
                cross(*pending.pop(0))
    while pending:
        cross(*pending.pop(0))
    for n in range(n_cols):
        total = own_sum(0, n)
        for t, owner in owners[:-1]:
            to_owner(t, owner, n).wait_recv()
            total = total + y_in[t - 1, :, cols(n)].astype(F32)
        o_ref[:, cols(n)] = total.astype(BF16)

    for buffer, sem in ((keys_in, k_send), (vals, v_send)):
        wait_for(buffer.reshape(n_seq * n_head, rows, HD).at[1:], sem)
    for t, owner in owners:
        sent = n_seq * CORES - (t == 0)
        wait_for(queries.reshape(n_seq * n_head, rows, HD).at[:sent], q_send.at[t])
        for cc in range(CORES):
            wait_for(att.at[t, cc, :, : (n_seq - 1) * HD], att_ssem.at[t, cc])
        for n in range(n_cols):
            to_pair(t, n).wait_send()
            if t > 0:
                to_owner(t, owner, n).wait_send()


def fused(n_seq, n_head, video_q, video_k, video_v, text_k, text_v, out_weight):
    rows, text = video_q.shape[0], text_k.shape[0]
    depth, d = out_weight.shape
    tokens = n_seq * n_head * rows
    chips = n_head // CORES
    per_chunk = next(c for c in (4, 2, 1) if n_seq % c == 0)
    chunks = n_seq // per_chunk
    m = per_chunk * rows
    n_cols = next(n for n in (4, 5, 8, 2, 1) if d % (n * 2 * HD) == 0)
    anywhere = pl.BlockSpec(memory_space=pl.ANY)
    dma = pltpu.SemaphoreType.DMA
    return pl.pallas_call(
        functools.partial(kernel, n_seq, n_head),
        out_shape=jax.ShapeDtypeStruct((rows, d), BF16),
        in_specs=[anywhere] * 6,
        out_specs=pl.BlockSpec(memory_space=pltpu.VMEM),
        scratch_shapes=[
            pltpu.VMEM((3, rows, video_q.shape[1]), BF16),
            pltpu.VMEM((n_seq, n_head, rows, HD), BF16),
            pltpu.VMEM((n_seq, n_head, rows, HD), BF16),
            pltpu.VMEM((n_seq, n_head, rows, HD), BF16),
            pltpu.VMEM((text, HD), BF16),
            pltpu.VMEM((text, HD), BF16),
            pltpu.VMEM((depth, d), BF16),
            pltpu.VMEM((chunks, m, tokens + text), BF16),
            pltpu.VMEM((chips, CORES, chunks, per_chunk, rows, HD), BF16),
            pltpu.VMEM((chips, CORES, rows, depth), BF16),
            pltpu.VMEM((chips, CORES, rows, d), BF16),
            pltpu.VMEM((chips, rows, d), BF16),
            pltpu.VMEM((max(chips - 1, 1), rows, d), BF16),
            pltpu.VMEM((max(chips - 1, 1), rows, d), BF16),
            dma((3,)), dma((2,)), dma((n_cols,)),
            dma(()), dma(()), dma(()), dma(()), dma((chips,)), dma((chips,)),
            dma((chips, CORES)), dma((chips, CORES)),
            dma((chips, n_cols)), dma((chips, n_cols)),
            dma((chips, n_cols)), dma((chips, n_cols)),
        ],
        compiler_params=pltpu.CompilerParams(
            collective_id=0, has_side_effects=True, vmem_limit_bytes=60 * 2**20
        ),
    )(video_q, video_k, video_v, text_k, text_v, out_weight)


def as_heads(array):
    return array.reshape(array.shape[0], array.shape[1] // HD, HD)


def scores_of(query_heads, key_heads):
    return jnp.einsum(
        "qhd,khd->hqk", query_heads, key_heads, preferred_element_type=jnp.float32
    ) * HD ** (-0.5)


def weigh_values(scores, row_max, value_heads):
    weights = jnp.exp(scores - row_max[..., None]).astype(jnp.bfloat16)
    totals = jnp.sum(weights.astype(jnp.float32), axis=2)
    summed = jnp.einsum("hqk,khd->hqd", weights, value_heads, preferred_element_type=jnp.float32)
    return (totals, summed)


def local_partial(query_heads, key_heads, value_heads):
    scores = scores_of(query_heads, key_heads)
    row_max = jnp.max(scores, axis=2)
    totals, summed = weigh_values(scores, row_max, value_heads)
    return (row_max, totals, summed)


def combine_partial(first, second):
    joint = jnp.maximum(first[0], second[0])
    first_factor = jnp.exp(first[0] - joint)
    second_factor = jnp.exp(second[0] - joint)
    totals = first[1] * first_factor + second[1] * second_factor
    summed = first[2] * first_factor[..., None] + second[2] * second_factor[..., None]
    return (joint, totals, summed)


def body(video_q, video_k, video_v, text_k, text_v, out_weight):
    queries, key_rows, value_rows = (
        lax.all_to_all(video_q, "head", split_axis=1, concat_axis=0, tiled=True),
        lax.all_to_all(video_k, "head", split_axis=1, concat_axis=0, tiled=True),
        lax.all_to_all(video_v, "head", split_axis=1, concat_axis=0, tiled=True),
    )
    rows_here = queries.shape[0]
    query_heads = as_heads(queries)
    text_part = local_partial(query_heads, as_heads(text_k), as_heads(text_v))
    merged = combine_partial(
        text_part,
        local_partial(
            query_heads,
            as_heads(lax.all_gather(key_rows, "seq", axis=0, tiled=True)),
            as_heads(lax.all_gather(value_rows, "seq", axis=0, tiled=True)),
        ),
    )
    normalized = merged[2] / merged[1][..., None]
    attended = normalized.transpose(1, 0, 2).reshape(rows_here, -1).astype(jnp.bfloat16)
    return lax.psum_scatter(
        jnp.dot(attended, out_weight, preferred_element_type=jnp.float32).astype(jnp.bfloat16),
        "head",
        scatter_dimension=0,
        tiled=True,
    )


def solution(mesh):
    n_seq, n_head = mesh.shape["seq"], mesh.shape["head"]

    def step(*arrays):
        heads_here = arrays[3].shape[1] // HD
        one_head_each = heads_here == n_seq and n_head % CORES == 0
        return fused(n_seq, n_head, *arrays) if one_head_each else body(*arrays)

    in_specs = (
        P(("seq", "head"), None),
        P(("seq", "head"), None),
        P(("seq", "head"), None),
        P(None, "head"),
        P(None, "head"),
        P("head", None),
    )
    out_specs = P(("seq", "head"), None)
    return jax.shard_map(step, mesh=mesh, in_specs=in_specs, out_specs=out_specs, check_vma=False)
```

profile of v0, /device:TPU:0, one launch (start us, length us, event | category | flops | bytes accessed | tf_op | source)
XLA Modules:
  0.0 43.6 jit_solution(8064258079572857990)
XLA Ops:
  0.0 41.8 %shard_map.64 = bf16[32,5120]{1,0:T(8,128)(2,1)} custom-call(bf16[32,4096]{1,0:T(8,128)(2,1)} %q_ref.1, bf16[32,4096]{1,0:T(8,128)(2,1)} %k_ref.1, bf16[32,4096]{1,0:T(8,128)(2,1)} %v_ref.1, bf16[512,1024]{1,0:T(8,128)(2,1)} %tk_ref.1, bf16[512,1024]{1,0:T(8,128)(2,1)} %tv_ref.1, bf16[1024,5120]{1,0:T(8,128)(2,1)} %w_ref.1), custom_call_target="tpu_custom_call" | custom-call | tf_op jit(solution)/shard_map/pallas_call | solution.py:222
  41.8 1.7 %copy.8 = bf16[32,5120]{1,0:T(8,128)(2,1)} copy(bf16[32,5120]{1,0:T(8,128)(2,1)} %shard_map.64) | data formatting | bytes 655360
where the time goes:
time: 43.7 us; the launch traced here: 43.6 us
  Pallas kernels  41.8 us (96%)
  local copies, waits for them, and re-layouts  1.72 us (4%)
    pallas_call x1, Pallas kernels, fused(): pl.pallas_call(functools.partial(kernel, n_seq, n_head), out_shape=jax.Sh...  41.8 us
    unnamed x1, local copies, waits for them, and re-layouts  1.72 us

commit v1 on v0

v1 whole, which is shorter than its diff:
```python
import functools
import itertools
import math

import jax
import jax.numpy as jnp
from jax import lax
from jax.experimental import pallas as pl
from jax.experimental.pallas import tpu as pltpu
from jax.sharding import PartitionSpec as P

HD = 128
BF16 = jnp.bfloat16
F32 = jnp.float32
CORES = 2
SIDES = 2
COLUMN = 2
LAG = 2
SCALE = HD ** (-0.5) * math.log2(math.e)


def kernel(
    n_seq, n_head, q_ref, k_ref, v_ref, tk_ref, tv_ref, w_ref, own_ref, pair_ref, far_ref,
    stage, keys_in, vals, queries, tk, tv, w, probs, att_send, stat_send, att, stat_in, mix, merged,
    acc, part, pair_in, y_send,
    load_sem, text_sem, w_sem, k_send, k_recv, v_send, v_recv, q_send, q_recv,
    att_ssem, att_rsem, stat_ssem, stat_rsem, pair_ssem, pair_rsem, y_ssem, y_rsem, own_sem, ready_sem,
):
    s, g = lax.axis_index("seq"), lax.axis_index("head")
    core, chip = lax.rem(g, CORES), lax.div(g, CORES)
    chips = n_head // CORES
    near = n_seq // SIDES
    side, seat = lax.div(s, near), lax.rem(s, near)
    rows, depth = q_ref.shape[0], w_ref.shape[0]
    n_cols = w_sem.shape[0]
    width = w_ref.shape[1] // n_cols
    halves, sub = att.shape[1], att.shape[4]
    wide = tk.shape[1]
    heads = wide // HD
    texts_here = tk.shape[0]
    m = CORES * sub
    split = near * n_head * rows

    def block(n):
        return pl.ds(pl.multiple_of(n * wide, wide), wide)

    def cols(n):
        return pl.ds(n * width, width)

    def part_of(r):
        return pl.ds(r * sub, sub)

    loads = [
        pltpu.make_async_copy(ref, stage.at[i], load_sem.at[i])
        for i, ref in enumerate((k_ref, v_ref, q_ref))
    ]
    my_text = pl.ds(pl.multiple_of(side * texts_here, texts_here), texts_here)
    texts = [
        pltpu.make_async_copy(tk_ref.at[my_text, block(seat)], tk, text_sem.at[0]),
        pltpu.make_async_copy(tv_ref.at[my_text, block(seat)], tv, text_sem.at[1]),
    ]
    weights = [
        pltpu.make_async_copy(w_ref.at[:, cols(n)], w.at[:, cols(n)], w_sem.at[n])
        for n in range(n_cols)
    ]
    for copy in loads + texts + weights:
        copy.start()

    turns = list(range(1, chips)) + [0]
    seat_z, seat_x = lax.div(seat, COLUMN), lax.rem(seat, COLUMN)
    inner = lax.rem(side + seat_z, SIDES) == 1
    outer = jnp.logical_not(inner)

    def device(across, oz, ox, turn, c):
        place = lax.rem(seat_z + oz, near // COLUMN) * COLUMN + lax.rem(seat_x + ox, COLUMN)
        ts = lax.rem(side + across, SIDES) * near + place
        return ts, lax.rem(chip + turn, chips) * CORES + lax.rem(core + c, CORES)

    def hops(across, oz, ox, turn, c):
        flat = ox + (turn > 0)
        if not across:
            return [(flat + oz, None)]
        if oz == 0:
            return [(flat + 2, None)]
        return [(flat + 1, inner), (flat + 3, outer)]

    def under(condition, action):
        if condition is None:
            action()
        else:
            pl.when(condition)(action)

    others = [
        where for where in itertools.product(
            (1, 0), range(near // COLUMN), range(COLUMN), turns, range(CORES)
        ) if any(where)
    ]
    reach = max(far for where in others for far, _ in hops(*where))

    def greet(semaphore, where):
        ts, tg = device(*where)
        pl.semaphore_signal(
            semaphore, inc=1, device_id={"seq": ts, "head": tg},
            device_id_type=pl.DeviceIdType.MESH,
        )

    def greet_adjacent(semaphore, some):
        always, within = 0, 0
        for where in others:
            for far, condition in hops(*where):
                if far <= 1 and some(where):
                    under(condition, functools.partial(greet, semaphore, where))
                    always, within = always + (condition is None), within + (condition is inner)
        pl.semaphore_wait(semaphore, always + jnp.where(inner, within, 0))

    greet_adjacent(pltpu.get_barrier_semaphore(), lambda where: True)

    def send(src, dst, ssem, rsem, ts, tg):
        return pltpu.make_async_remote_copy(
            src_ref=src, dst_ref=dst, send_sem=ssem, recv_sem=rsem,
            device_id={"seq": ts, "head": tg}, device_id_type=pl.DeviceIdType.MESH,
        )

    def wait_for(ref, sem):
        pltpu.make_async_copy(ref, ref, sem).wait()

    def owned(ts, tg):
        return block(tg * near + lax.rem(ts, near))

    mine = owned(s, g)

    def give(i, chosen, dst, ssem, rsem, where):
        ts, tg = device(*where)
        send(stage.at[i, chosen, owned(ts, tg)], dst, ssem, rsem, ts, tg).start()

    def give_query(r, where):
        turn = where[3]
        give(
            2, part_of(r), queries.at[s, g, part_of(r)],
            q_send.at[turn, r], q_recv.at[turn, r], where,
        )

    for copy in loads:
        copy.wait()
    given = set()
    everything = pl.ds(0, rows)
    for known in range(1, reach + 1):
        if known > 1:
            greet_adjacent(ready_sem.at[known - 2], lambda where: where[4] == 0)
        now = [
            (where, condition) for where in others for far, condition in hops(*where)
            if far == known or known == 1 and far == 0
        ]
        for i, (buffer, ssem, rsem) in enumerate(((keys_in, k_send, k_recv), (vals, v_send, v_recv))):
            for where, condition in now:
                if not where[0]:
                    give(i, everything, buffer.at[seat, g], ssem, rsem, where)
        for r in range(halves):
            for where, condition in now:
                if where[3] > 0 or condition is inner:
                    under(condition, functools.partial(give_query, r, where))
                    given.add((r, where, condition is outer))
    for r in range(halves):
        for where in others:
            for far, condition in hops(*where):
                if (r, where, condition is outer) not in given:
                    under(condition, functools.partial(give_query, r, where))
    pltpu.make_async_copy(stage.at[0, :, mine], keys_in.at[seat, g], k_recv).start()
    pltpu.make_async_copy(stage.at[1, :, mine], vals.at[seat, g], v_recv).start()
    for r in range(halves):
        pltpu.make_async_copy(
            stage.at[2, part_of(r), mine], queries.at[s, g, part_of(r)], q_recv.at[0, r]
        ).start()

    for copy in texts:
        copy.wait()
    wait_for(keys_in, k_recv)
    wait_for(vals, v_recv)
    keyed = (((1,), (1,)), ((), ()))
    owners = [(t, lax.rem(chip + t, chips)) for t in turns]
    passes = [(t, owner, r) for t, owner in owners for r in range(halves)]
    count = near * m
    lane = lax.broadcasted_iota(jnp.int32, (count, HD), 1)

    def lanes(h):
        return pl.ds(h * HD, HD)

    def deliver(t, r, c, b):
        here = lax.rem(seat + 1 + b, near)
        pieces = (
            (
                att_send.at[t, r, c, here], att.at[t, r, side, :, :, block(seat)],
                att_ssem.at[t, r], att_rsem.at[t, r, seat],
            ),
            (
                stat_send.at[t, r, c], stat_in.at[t, r, side, seat],
                stat_ssem.at[t, r], stat_rsem.at[t, r, seat],
            ),
        )
        for src, dst, ssem, rsem in pieces:
            if c == SIDES - 1 and b == near - 1:
                pltpu.make_async_copy(src, dst, rsem).start()
            else:
                to_side = lax.rem(side + c + 1, SIDES)
                send(src, dst, ssem, rsem, to_side * near + here, g).start()

    for t, owner, r in passes:
        chosen = pl.ds(owner * CORES, CORES)
        wait_for(queries.at[:, chosen, part_of(r)], q_recv.at[t, r])
        for c in range(SIDES):
            to_side = lax.rem(side + c + 1, SIDES)
            first = to_side * near
            tops = []
            for h in range(heads):
                q = queries[pl.ds(first, near), chosen, part_of(r), lanes(h)].reshape(count, HD)
                keys = keys_in[:, :, :, lanes(h)].reshape(split, HD)
                on_video = lax.dot_general(q, keys, keyed, preferred_element_type=F32)
                on_text = lax.dot_general(q, tk[:, lanes(h)], keyed, preferred_element_type=F32)
                top = jnp.maximum(
                    jnp.max(on_video, axis=1, keepdims=True),
                    jnp.max(on_text, axis=1, keepdims=True),
                )
                probs[c, h, :, :split] = jnp.exp2((on_video - top) * SCALE).astype(BF16)
                probs[c, h, :, split:] = jnp.exp2((on_text - top) * SCALE).astype(BF16)
                tops.append(top)
            logs = None
            for h in range(heads):
                values, words = vals[:, :, :, lanes(h)].reshape(split, HD), tv[:, lanes(h)]
                ahead = jnp.dot(
                    probs[c, h, :, :split],
                    jnp.concatenate([values, jnp.ones_like(values)], axis=1),
                    preferred_element_type=F32,
                ) + jnp.dot(
                    probs[c, h, :, split:],
                    jnp.concatenate([words, jnp.ones_like(words)], axis=1),
                    preferred_element_type=F32,
                )
                total = ahead[:, HD:]
                done = (ahead[:, :HD] / total).astype(BF16)
                att_send[t, r, c, :, :, :, lanes(h)] = done.reshape(near, CORES, sub, HD)
                log = tops[h] * SCALE + jnp.log2(total)
                logs = log if h == 0 else jnp.where(lane < h * (HD // heads), logs, log)
            turned = logs.T
            for h in range(heads):
                at = h * (HD // heads)
                stat_send[t, r, c, h : h + 1, :] = turned[at : at + 1, :]
            if t > 0:
                for b in range(near):
                    deliver(t, r, c, b)
    for b in range(near):
        for r in range(halves):
            for c in range(SIDES):
                deliver(0, r, c, b)

    def merge(t, r, n):
        wait_for(att.at[t, r, :, :, :, block(n)], att_rsem.at[t, r, n])
        wait_for(stat_in.at[t, r, :, n], stat_rsem.at[t, r, n])
        weight = 1.0 / (1.0 + jnp.exp2(stat_in[t, r, 1, n] - stat_in[t, r, 0, n]))
        weight = jnp.concatenate(
            [jnp.broadcast_to(weight[h : h + 1], (HD // heads, count)) for h in range(heads)], axis=0
        ).T
        mix[t, r, n] = weight
        mine = mix[t, r, n, pl.ds(pl.multiple_of(seat * m, m), m), :]
        out = []
        for h in range(heads):
            at = h * (HD // heads)
            held = [
                att[t, r, i, :, :, pl.ds(pl.multiple_of(n * wide + h * HD, HD), HD)]
                .reshape(m, HD).astype(F32)
                for i in range(SIDES)
            ]
            out.append((held[1] + (held[0] - held[1]) * mine[:, at : at + 1]).astype(BF16))
        return jnp.concatenate(out, axis=1)

    def to_pair(t, r, n):
        landing = pair_ref.at[part_of(r), cols(n)] if t == 0 else pair_in.at[t - 1, r, :, cols(n)]
        return send(
            part.at[t, r, 1 - core, :, cols(n)], landing,
            pair_ssem.at[t, r, n], pair_rsem.at[t, r, n], s, g + 1 - 2 * core,
        )

    def to_owner(t, r, owner, n):
        return send(
            y_send.at[t - 1, r, :, cols(n)], far_ref.at[t - 1, part_of(r), cols(n)],
            y_ssem.at[t - 1, r, n], y_rsem.at[t - 1, r, n], s, owner * CORES + core,
        )

    def to_own(r, n):
        return pltpu.make_async_copy(
            part.at[0, r, core, :, cols(n)], own_ref.at[part_of(r), cols(n)], own_sem.at[r, n]
        )

    def cross(t, r, owner, n):
        to_pair(t, r, n).wait_recv()
        total = part[t, r, core, :, cols(n)].astype(F32) + pair_in[t - 1, r, :, cols(n)].astype(F32)
        y_send[t - 1, r, :, cols(n)] = total.astype(BF16)
        to_owner(t, r, owner, n).start()

    pending = []
    for copy in weights:
        copy.wait()
    for t, owner in owners[:-1]:
        for r in range(halves):
            for n in range(near):
                merged[t, r, :, n * wide : (n + 1) * wide] = merge(t, r, n)
            for n in range(n_cols):
                made = jnp.dot(merged[t, r], w[:, cols(n)], preferred_element_type=F32)
                part[t, r, :, :, cols(n)] = made.astype(BF16).reshape(CORES, sub, width)
                to_pair(t, r, n).start()
                pending.append((t, r, owner, n))
                if len(pending) > LAG:
                    cross(*pending.pop(0))
    while pending:
        cross(*pending.pop(0))
    for step in range(near):
        z = lax.rem(seat + 2 * near - 1 - step, near)
        both = jnp.concatenate([merge(0, r, z) for r in range(halves)], axis=0)
        for n in range(n_cols):
            made = jnp.dot(both, w[block(z), cols(n)], preferred_element_type=F32)
            if step > 0:
                made = made + acc[:, cols(n)]
            if step < near - 1:
                acc[:, cols(n)] = made
            else:
                part[0, :, :, :, cols(n)] = made.astype(BF16).reshape(halves, CORES, sub, width)
                for r in range(halves):
                    to_pair(0, r, n).start()
                    to_own(r, n).start()
            if pending:
                cross(*pending.pop(0))
    while pending:
        cross(*pending.pop(0))
    for buffer, sem in ((keys_in, k_send), (vals, v_send)):
        wait_for(buffer.reshape(near * n_head, rows, wide).at[1:], sem)
    for t, owner in owners:
        sent = n_seq * CORES - (t == 0)
        for r in range(halves):
            wait_for(
                queries.reshape(n_seq * n_head, rows, wide).at[:sent, part_of(r)], q_send.at[t, r]
            )
            wait_for(
                att_send.at[t, r].reshape(n_seq, CORES, sub, wide).at[1:], att_ssem.at[t, r]
            )
            wait_for(stat_in.at[t, r].reshape(n_seq, heads, count).at[1:], stat_ssem.at[t, r])
            for n in range(n_cols):
                to_pair(t, r, n).wait_send()
                if t > 0:
                    to_owner(t, r, owner, n).wait()
                else:
                    to_pair(t, r, n).wait_recv()
                    to_own(r, n).wait()


def fused(n_seq, n_head, video_q, video_k, video_v, text_k, text_v, out_weight):
    rows, text = video_q.shape[0], text_k.shape[0]
    depth, d = out_weight.shape
    near = n_seq // SIDES
    wide = text_k.shape[1] // near
    heads = wide // HD
    chips = n_head // CORES
    halves = 2 if rows % 32 == 0 else 1
    sub = rows // halves
    count = near * CORES * sub
    keys = near * n_head * rows + text // SIDES
    n_cols = next(n for n in (4, 5, 8, 2, 1) if d % (n * 2 * HD) == 0)
    anywhere = pl.BlockSpec(memory_space=pl.ANY)
    dma = pltpu.SemaphoreType.DMA
    far = max(chips - 1, 1)
    own, pair, across = pl.pallas_call(
        functools.partial(kernel, n_seq, n_head),
        out_shape=(
            jax.ShapeDtypeStruct((rows, d), BF16),
            jax.ShapeDtypeStruct((rows, d), BF16),
            jax.ShapeDtypeStruct((far, rows, d), BF16),
        ),
        in_specs=[anywhere] * 6,
        out_specs=(anywhere,) * 3,
        scratch_shapes=[
            pltpu.VMEM((3, rows, video_q.shape[1]), BF16),
            pltpu.VMEM((near, n_head, rows, wide), BF16),
            pltpu.VMEM((near, n_head, rows, wide), BF16),
            pltpu.VMEM((n_seq, n_head, rows, wide), BF16),
            pltpu.VMEM((text // SIDES, wide), BF16),
            pltpu.VMEM((text // SIDES, wide), BF16),
            pltpu.VMEM((depth, d), BF16),
            pltpu.VMEM((SIDES, heads, count, keys), BF16),
            pltpu.VMEM((chips, halves, SIDES, near, CORES, sub, wide), BF16),
            pltpu.VMEM((chips, halves, SIDES, heads, count), F32),
            pltpu.VMEM((chips, halves, SIDES, CORES, sub, depth), BF16),
            pltpu.VMEM((chips, halves, SIDES, near, heads, count), F32),
            pltpu.VMEM((chips, halves, near, count, HD), F32),
            pltpu.VMEM((chips, halves, CORES * sub, depth), BF16),
            pltpu.VMEM((rows * CORES, d), F32),
            pltpu.VMEM((chips, halves, CORES, sub, d), BF16),
            pltpu.VMEM((far, halves, sub, d), BF16),
            pltpu.VMEM((far, halves, sub, d), BF16),
            dma((3,)), dma((2,)), dma((n_cols,)),
            dma(()), dma(()), dma(()), dma(()), dma((chips, halves)), dma((chips, halves)),
            dma((chips, halves)), dma((chips, halves, near)),
            dma((chips, halves)), dma((chips, halves, near)),
            dma((chips, halves, n_cols)), dma((chips, halves, n_cols)),
            dma((far, halves, n_cols)), dma((far, halves, n_cols)), dma((halves, n_cols)),
            pltpu.SemaphoreType.REGULAR((n_seq,)),
        ],
        compiler_params=pltpu.CompilerParams(
            collective_id=0, has_side_effects=True, vmem_limit_bytes=60 * 2**20
        ),
    )(video_q, video_k, video_v, text_k, text_v, out_weight)
    total = own.astype(F32) + pair.astype(F32)
    for t in range(chips - 1):
        total = total + across[t].astype(F32)
    return total.astype(BF16)


def as_heads(array):
    return array.reshape(array.shape[0], array.shape[1] // HD, HD)


def scores_of(query_heads, key_heads):
    return jnp.einsum(
        "qhd,khd->hqk", query_heads, key_heads, preferred_element_type=jnp.float32
    ) * HD ** (-0.5)


def weigh_values(scores, row_max, value_heads):
    weights = jnp.exp(scores - row_max[..., None]).astype(jnp.bfloat16)
    totals = jnp.sum(weights.astype(jnp.float32), axis=2)
    summed = jnp.einsum("hqk,khd->hqd", weights, value_heads, preferred_element_type=jnp.float32)
    return (totals, summed)


def local_partial(query_heads, key_heads, value_heads):
    scores = scores_of(query_heads, key_heads)
    row_max = jnp.max(scores, axis=2)
    totals, summed = weigh_values(scores, row_max, value_heads)
    return (row_max, totals, summed)


def combine_partial(first, second):
    joint = jnp.maximum(first[0], second[0])
    first_factor = jnp.exp(first[0] - joint)
    second_factor = jnp.exp(second[0] - joint)
    totals = first[1] * first_factor + second[1] * second_factor
    summed = first[2] * first_factor[..., None] + second[2] * second_factor[..., None]
    return (joint, totals, summed)


def body(video_q, video_k, video_v, text_k, text_v, out_weight):
    queries, key_rows, value_rows = (
        lax.all_to_all(video_q, "head", split_axis=1, concat_axis=0, tiled=True),
        lax.all_to_all(video_k, "head", split_axis=1, concat_axis=0, tiled=True),
        lax.all_to_all(video_v, "head", split_axis=1, concat_axis=0, tiled=True),
    )
    rows_here = queries.shape[0]
    query_heads = as_heads(queries)
    text_part = local_partial(query_heads, as_heads(text_k), as_heads(text_v))
    merged = combine_partial(
        text_part,
        local_partial(
            query_heads,
            as_heads(lax.all_gather(key_rows, "seq", axis=0, tiled=True)),
            as_heads(lax.all_gather(value_rows, "seq", axis=0, tiled=True)),
        ),
    )
    normalized = merged[2] / merged[1][..., None]
    attended = normalized.transpose(1, 0, 2).reshape(rows_here, -1).astype(jnp.bfloat16)
    return lax.psum_scatter(
        jnp.dot(attended, out_weight, preferred_element_type=jnp.float32).astype(jnp.bfloat16),
        "head",
        scatter_dimension=0,
        tiled=True,
    )


def solution(mesh):
    n_seq, n_head = mesh.shape["seq"], mesh.shape["head"]

    def step(*arrays):
        heads_here = arrays[3].shape[1] // HD
        paired = heads_here == n_seq and n_head % CORES == 0 and n_head == 2 * CORES and n_seq == 2 * SIDES * COLUMN
        tiled = n_seq // SIDES * CORES * arrays[0].shape[0] == 2 * HD
        return fused(n_seq, n_head, *arrays) if paired and tiled else body(*arrays)

    in_specs = (
        P(("seq", "head"), None),
        P(("seq", "head"), None),
        P(("seq", "head"), None),
        P(None, "head"),
        P(None, "head"),
        P("head", None),
    )
    out_specs = P(("seq", "head"), None)
    return jax.shard_map(step, mesh=mesh, in_specs=in_specs, out_specs=out_specs, check_vma=False)
```

time: 43.7 us -> 42.4 us (0.970)
  other arithmetic: 0 us -> 2.02 us
  local copies, waits for them, and re-layouts: 1.72 us -> 0 us
  Pallas kernels: 41.8 us -> 40.3 us
    convert_element_type x0 -> x1, other arithmetic: none -> 2.02 us  [fused(): return total.astype(BF16)]
    unnamed x1 -> x0, local copies, waits for them, and re-layouts: 1.72 us -> none
    pallas_call x1, Pallas kernels: 41.8 us -> 40.3 us  [fused(): pl.pallas_call(functools.partial(kernel, n_seq, n_head), out_shape=(jax.S...]
where the time goes in v1:
time: 42.4 us; the launch traced here: 42.3 us
  Pallas kernels  40.3 us (95%)
  other arithmetic  2.02 us (5%)
    pallas_call x1, Pallas kernels, fused(): pl.pallas_call(functools.partial(kernel, n_seq, n_head), out_shape=(jax.S...  40.3 us
    convert_element_type x1, other arithmetic, fused(): return total.astype(BF16)  2.02 us

profile of v1, /device:TPU:0, one launch (start us, length us, event | category | flops | bytes accessed | tf_op | source)
XLA Modules:
  0.0 42.3 jit_solution(14326310821455323435)
XLA Ops:
  0.0 40.3 %shard_map.64 = (bf16[32,5120]{1,0:T(8,128)(2,1)}, bf16[32,5120]{1,0:T(8,128)(2,1)}, bf16[1,32,5120]{2,1,0:T(8,128)(2,1)}) custom-call(bf16[32,4096]{1,0:T(8,128)(2,1)} %q_ref.1, bf16[32,4096]{1,0:T(8,128)(2,1)} %k_ref.1, bf16[32,4096]{1,0:T(8,128)(2,1)} %v_ref.1, bf16[512,1024]{1,0:T(8,128)(2,1)} %tk_ref.1, bf16[512,1024]{1,0:T(8,128)(2,1)} %tv_ref.1, ...), custom_call_target="tpu_custom_call" | custom-call | tf_op jit(solution)/shard_map/pallas_call | solution.py:369
  40.3 2.0 %fusion = bf16[32,5120]{1,0:T(8,128)(2,1)} fusion(bf16[32,5120]{1,0:T(8,128)(2,1)} %get-tuple-element.9, bf16[32,5120]{1,0:T(8,128)(2,1)} %get-tuple-element.8, bf16[1,32,5120]{2,1,0:T(8,128)(2,1)} %get-tuple-element.10), kind=kLoop, calls=%fused_computation.1 | loop fusion | flops 983040 | bytes 1310720 | tf_op jit(solution)/shard_map/convert_element_type | solution.py:412

commit v2 on v1

--- a/solution.py
+++ b/solution.py
@@ -151,20 +151,21 @@
             (where, condition) for where in others for far, condition in hops(*where)
             if far == known or known == 1 and far == 0
         ]
-        for i, (buffer, ssem, rsem) in enumerate(((keys_in, k_send, k_recv), (vals, v_send, v_recv))):
-            for where, condition in now:
-                if not where[0]:
-                    give(i, everything, buffer.at[seat, g], ssem, rsem, where)
+        for where, condition in now:
+            if not where[0]:
+                give(0, everything, keys_in.at[seat, g], k_send, k_recv, where)
+                give(1, everything, vals.at[seat, g], v_send, v_recv, where)
         for r in range(halves):
             for where, condition in now:
-                if where[3] > 0 or condition is inner:
+                if condition is inner:
                     under(condition, functools.partial(give_query, r, where))
                     given.add((r, where, condition is outer))
-    for r in range(halves):
-        for where in others:
-            for far, condition in hops(*where):
-                if (r, where, condition is outer) not in given:
-                    under(condition, functools.partial(give_query, r, where))
+    urgent = [(r, where) for r in range(halves) for where in others if where[3] > 0]
+    others_last = [(r, where) for where in others for r in range(halves) if where[3] == 0]
+    for r, where in urgent + others_last:
+        for far, condition in hops(*where):
+            if (r, where, condition is outer) not in given:
+                under(condition, functools.partial(give_query, r, where))
     pltpu.make_async_copy(stage.at[0, :, mine], keys_in.at[seat, g], k_recv).start()
     pltpu.make_async_copy(stage.at[1, :, mine], vals.at[seat, g], v_recv).start()
     for r in range(halves):

time: 42.4 us -> 41.8 us (0.986)
  Pallas kernels: 40.3 us -> 39.6 us
    pallas_call x1, Pallas kernels: 40.3 us -> 39.6 us  [fused(): pl.pallas_call(functools.partial(kernel, n_seq, n_head), out_shape=(jax.S...]
where the time goes in v2:
time: 41.8 us; the launch traced here: 41.6 us
  Pallas kernels  39.6 us (95%)
  other arithmetic  2.02 us (5%)
    pallas_call x1, Pallas kernels, fused(): pl.pallas_call(functools.partial(kernel, n_seq, n_head), out_shape=(jax.S...  39.6 us
    convert_element_type x1, other arithmetic, fused(): return total.astype(BF16)  2.02 us

profile of v2, /device:TPU:0, one launch (start us, length us, event | category | flops | bytes accessed | tf_op | source)
XLA Modules:
  0.0 41.6 jit_solution(3328260561721704243)
XLA Ops:
  0.0 39.6 %shard_map.64 = (bf16[32,5120]{1,0:T(8,128)(2,1)}, bf16[32,5120]{1,0:T(8,128)(2,1)}, bf16[1,32,5120]{2,1,0:T(8,128)(2,1)}) custom-call(bf16[32,4096]{1,0:T(8,128)(2,1)} %q_ref.1, bf16[32,4096]{1,0:T(8,128)(2,1)} %k_ref.1, bf16[32,4096]{1,0:T(8,128)(2,1)} %v_ref.1, bf16[512,1024]{1,0:T(8,128)(2,1)} %tk_ref.1, bf16[512,1024]{1,0:T(8,128)(2,1)} %tv_ref.1, ...), custom_call_target="tpu_custom_call" | custom-call | tf_op jit(solution)/shard_map/pallas_call | solution.py:370
  39.6 2.0 %fusion = bf16[32,5120]{1,0:T(8,128)(2,1)} fusion(bf16[32,5120]{1,0:T(8,128)(2,1)} %get-tuple-element.9, bf16[32,5120]{1,0:T(8,128)(2,1)} %get-tuple-element.8, bf16[1,32,5120]{2,1,0:T(8,128)(2,1)} %get-tuple-element.10), kind=kLoop, calls=%fused_computation.1 | loop fusion | flops 983040 | bytes 1310720 | tf_op jit(solution)/shard_map/convert_element_type | solution.py:413

commit v3 on v2

--- a/solution.py
+++ b/solution.py
@@ -198,12 +198,14 @@
                 stat_ssem.at[t, r], stat_rsem.at[t, r, seat],
             ),
         )
-        for src, dst, ssem, rsem in pieces:
+        for src, dst, ssem, rsem in pieces[::-1]:
             if c == SIDES - 1 and b == near - 1:
                 pltpu.make_async_copy(src, dst, rsem).start()
             else:
                 to_side = lax.rem(side + c + 1, SIDES)
-                send(src, dst, ssem, rsem, to_side * near + here, g).start()
+                parts = [(src.at[e], dst.at[e]) for e in range(CORES)] if len(src.shape) == 3 else [(src, dst)]
+                for one, other in parts:
+                    send(one, other, ssem, rsem, to_side * near + here, g).start()
 
     for t, owner, r in passes:
         chosen = pl.ds(owner * CORES, CORES)

time: 41.8 us -> 41.7 us (level)
  no operation moved by 1% of the time
where the time goes in v3:
time: 41.7 us; the launch traced here: 41.6 us
  Pallas kernels  39.6 us (95%)
  other arithmetic  2.02 us (5%)
    pallas_call x1, Pallas kernels, fused(): pl.pallas_call(functools.partial(kernel, n_seq, n_head), out_shape=(jax.S...  39.6 us
    convert_element_type x1, other arithmetic, fused(): return total.astype(BF16)  2.02 us

profile of v3, /device:TPU:0, one launch (start us, length us, event | category | flops | bytes accessed | tf_op | source)
XLA Modules:
  0.0 41.6 jit_solution(7033390163571384391)
XLA Ops:
  0.0 39.6 %shard_map.64 = (bf16[32,5120]{1,0:T(8,128)(2,1)}, bf16[32,5120]{1,0:T(8,128)(2,1)}, bf16[1,32,5120]{2,1,0:T(8,128)(2,1)}) custom-call(bf16[32,4096]{1,0:T(8,128)(2,1)} %q_ref.1, bf16[32,4096]{1,0:T(8,128)(2,1)} %k_ref.1, bf16[32,4096]{1,0:T(8,128)(2,1)} %v_ref.1, bf16[512,1024]{1,0:T(8,128)(2,1)} %tk_ref.1, bf16[512,1024]{1,0:T(8,128)(2,1)} %tv_ref.1, ...), custom_call_target="tpu_custom_call" | custom-call | tf_op jit(solution)/shard_map/pallas_call | solution.py:372
  39.6 2.0 %fusion = bf16[32,5120]{1,0:T(8,128)(2,1)} fusion(bf16[32,5120]{1,0:T(8,128)(2,1)} %get-tuple-element.9, bf16[32,5120]{1,0:T(8,128)(2,1)} %get-tuple-element.8, bf16[1,32,5120]{2,1,0:T(8,128)(2,1)} %get-tuple-element.10), kind=kLoop, calls=%fused_computation.1 | loop fusion | flops 983040 | bytes 1310720 | tf_op jit(solution)/shard_map/convert_element_type | solution.py:415
